TPU v7x, 256 devices: a whole 4x4x8 slice. The times are simulated.
256 devices in a mesh: blk: 32 (over y_lo, z, core), tp: 8 (over x, y_hi).
Axes of the slice: x: 4, y: 4 (y_hi: 2, y_lo: 2; y = y_hi * 2 + y_lo), z: 8, core: 2. Of those that a mesh axis runs over, the one named last changes fastest.
Arguments:
- dec_states: bfloat16 [8192, 5120], P('blk', 'tp'), may hold values from -200 to 200
- norm_gain: float32 [5120], replicated, may hold values from 0.1 to 1.9
- query_weight: bfloat16 [5120, 3072], P(None, 'tp'), may hold values from -0.078125 to 0.078125
- out_weight: bfloat16 [3072, 5120], P('tp'), may hold values from -0.109375 to 0.109375
- enc_keys: bfloat16 [12288, 3072], P('blk', 'tp'), may hold values from -1000 to 1000
- enc_values: bfloat16 [12288, 3072], P('blk', 'tp'), may hold values from -6 to 6
Outputs:
- attn_out: bfloat16 [8192, 5120], P('blk', 'tp')
All inputs are finite; a program needn't handle non-finite values.
Results may differ from a plain program's by a relative error of at most 0.034.
Values may be sent and summed in bfloat16 or wider, within the bound.
A program may use at most 128 MiB of HBM per device.

v0:
```python
import math

import jax
import jax.numpy as jnp
from jax import lax
from jax.sharding import PartitionSpec as P

HEAD_DIM = 128


NORM_EPS = 1e-06


def sent_to_all(array, axis):
    devices = lax.axis_size(axis)
    return lax.all_to_all(
        jnp.broadcast_to(array[None], (devices, *array.shape)), axis, 0, 0, tiled=True
    )


def in_order(parts, dim):
    shape = list(parts.shape[1:])
    shape[dim] *= parts.shape[0]
    return jnp.moveaxis(parts, 0, dim).reshape(shape)


def gathered_copies(array, axis, dim):
    parts = sent_to_all(array, axis)
    return in_order(parts, dim)


def in_one_piece(arrays, axis, dim, along):
    ends, at = ([], 0)
    for a in arrays[:-1]:
        at += a.shape[along]
        ends.append(at)
    both = jnp.concatenate(arrays, axis=along)
    return tuple(jnp.split(lax.all_gather(both, axis, axis=dim, tiled=True), ends, axis=along))


def block_rows(total_rows, shard_rows, limit):
    shards = total_rows // shard_rows
    chosen = 1
    for count_try in range(1, shards + 1):
        if shards % count_try == 0 and count_try * shard_rows <= limit:
            chosen = count_try
    return chosen * shard_rows


def per_device(dec_states, norm_gain, query_weight, out_weight, enc_keys, enc_values):
    heads = query_weight.shape[1] // HEAD_DIM
    q_rows = dec_states.shape[0]
    score_scale = 1.0 / math.sqrt(HEAD_DIM)
    states = gathered_copies(dec_states, "tp", 1).astype(jnp.float32)
    mean_sq = jnp.mean(states * states, axis=1, keepdims=True)
    normed = (states * lax.rsqrt(mean_sq + NORM_EPS) * norm_gain).astype(jnp.bfloat16)
    queries = jnp.dot(normed, query_weight, preferred_element_type=jnp.float32).astype(jnp.bfloat16)
    query_heads = queries.reshape(q_rows, heads, HEAD_DIM)
    shard_rows = enc_keys.shape[0]
    start_state = (
        jnp.full((heads, q_rows), -1e30, jnp.float32),
        jnp.zeros((heads, q_rows), jnp.float32),
        jnp.zeros((heads, q_rows, HEAD_DIM), jnp.float32),
    )
    key_rows, value_rows = in_one_piece((enc_keys, enc_values), "blk", 0, 1)
    count = key_rows.shape[0]
    width_rows = block_rows(count, shard_rows, 1536)
    key_blocks = key_rows.reshape(count // width_rows, width_rows, heads, HEAD_DIM)
    value_blocks = value_rows.reshape(count // width_rows, width_rows, heads, HEAD_DIM)

    def step_block(state, blocks):
        row_max, row_sum, summed = state
        key_block, value_block = blocks
        scores = (
            jnp.einsum("qhd,khd->hqk", query_heads, key_block, preferred_element_type=jnp.float32)
            * score_scale
        )
        new_max = jnp.maximum(row_max, jnp.max(scores, axis=2))
        factor = jnp.exp(row_max - new_max)
        exp_scores = jnp.exp(scores - new_max[:, :, None])
        new_sum = row_sum * factor + jnp.sum(exp_scores, axis=2)
        mixed = jnp.einsum(
            "hqk,khd->hqd",
            exp_scores.astype(jnp.bfloat16),
            value_block,
            preferred_element_type=jnp.float32,
        )
        return ((new_max, new_sum, summed * factor[:, :, None] + mixed), None)

    result, unused = lax.scan(step_block, start_state, (key_blocks, value_blocks))
    row_max, row_sum, summed = result
    attended = (
        (summed / row_sum[:, :, None])
        .transpose(1, 0, 2)
        .reshape(q_rows, heads * HEAD_DIM)
        .astype(jnp.bfloat16)
    )
    partial_out = jnp.dot(attended, out_weight, preferred_element_type=jnp.float32)
    return lax.psum_scatter(partial_out.astype(jnp.bfloat16), "tp", scatter_dimension=1, tiled=True)


def solution(mesh):
    in_specs = (P("blk", "tp"), P(), P(None, "tp"), P("tp", None), P("blk", "tp"), P("blk", "tp"))
    out_specs = P("blk", "tp")
    return jax.shard_map(
        per_device, mesh=mesh, in_specs=in_specs, out_specs=out_specs, check_vma=False
    )
```

profile of v0, /device:TPU:1, one launch (start us, length us, event | category | flops | bytes accessed | tf_op | source)
XLA Modules:
  0.0 413.9 jit_solution(526484908211751444)
XLA Ops:
  6.5 1.9 pad_maximum_fusion
  8.5 1.1 copy.20
  9.6 1.7 broadcast_in_dim.13
  11.3 7.5 %all-to-all-start = ((bf16[8,256,640]{1,2,0:T(8,128)(2,1)}), bf16[8,256,640]{1,2,0:T(8,128)(2,1)S(1)}, u32[]{:S(2)}, u32[]{:S(2)}) async-start(bf16[8,256,640]{1,2,0:T(8,128)(2,1)} %broadcast_in_dim.13), calls=%async_computation | async-start | bytes 5242880 | tf_op jit(solution)/shard_map/all_to_all | solution.py:16
  18.8 37.7 %all-to-all-done = bf16[8,256,640]{1,2,0:T(8,128)(2,1)S(1)} async-done(((bf16[8,256,640]{1,2,0:T(8,128)(2,1)}), bf16[8,256,640]{1,2,0:T(8,128)(2,1)S(1)}, u32[]{:S(2)}, u32[]{:S(2)}) %all-to-all-start) | async-done | bytes 2621472 | tf_op jit(solution)/shard_map/all_to_all | solution.py:16
  56.6 0.7 multiply_reduce_fusion
  57.3 2.2 fusion.20
  59.5 1.6 convolution_convert_fusion.1
  61.4 83.9 %all-gather.2.cloned.1.call-done = bf16[12288,768]{1,0:T(8,128)(2,1)} async-done(((bf16[384,768]{1,0:T(8,128)(2,1)}), bf16[12288,768]{1,0:T(8,128)(2,1)}) %all-gather.2.cloned.1.call-update) | async-done | bytes 18874384 | tf_op jit(solution)/shard_map/all_gather | solution.py:38
  145.3 15.0 %fusion.21 = (bf16[12288,384]{1,0:T(8,128)(2,1)}, bf16[12288,384]{1,0:T(8,128)(2,1)}) fusion(bf16[12288,768]{1,0:T(8,128)(2,1)} %all-gather.2.cloned.1.call-done), kind=kLoop, calls=%fused_computation.31 | loop fusion | bytes 37748736 | tf_op jit(solution)/shard_map/split | solution.py:38
  160.3 24.5 %reshape.31 = bf16[8,1536,3,128]{3,2,1,0:T(4,128)(2,1)} reshape(bf16[12288,384]{1,0:T(8,128)(2,1)} %get-tuple-element.109) | data formatting | bytes 18874368 | tf_op jit(solution)/shard_map/reshape | solution.py:68
  184.7 10.6 %copy.23 = bf16[8,1536,3,128]{3,1,2,0:T(8,128)(2,1)} copy(bf16[8,1536,3,128]{3,2,1,0:T(4,128)(2,1)} %reshape.31) | data formatting | bytes 18874368
  195.3 24.5 %reshape.32 = bf16[8,1536,3,128]{3,2,1,0:T(4,128)(2,1)} reshape(bf16[12288,384]{1,0:T(8,128)(2,1)} %get-tuple-element.108) | data formatting | bytes 18874368 | tf_op jit(solution)/shard_map/reshape | solution.py:69
  219.8 10.7 %copy.25 = bf16[8,1536,3,128]{3,1,2,0:T(8,128)(2,1)} copy(bf16[8,1536,3,128]{3,2,1,0:T(4,128)(2,1)} %reshape.32) | data formatting | bytes 18874368
  230.5 83.9 %while.15 = (s32[]{:T(128)}, f32[3,256]{1,0:T(4,128)S(1)}, f32[3,256]{1,0:T(4,128)S(1)}, f32[3,256,128]{2,1,0:T(8,128)S(1)}, bf16[8,1536,3,128]{3,1,2,0:T(8,128)...) while((s32[]{:T(128)}, f32[3,256]{1,0:T(4,128)S(1)}, ...), condition=%wide.region_4.5_spmd.clone, body=%wide.region_1.4_spmd.clone.sunk | while | flops 613715712 | bytes 36422788 | solution.py:90
  230.5 4.2 %bitcast_reduce_fusion.2 = (f32[3,256]{1,0:T(4,128)S(1)}, f32[3,1536,256]{2,1,0:T(8,128)}) fusion(bf16[256,3,128]{2,0,1:T(8,128)(2,1)S(1)} %get-tuple-element.184, bf16[8,1536,3,128]{3,1,2,0:T(8,128)(2,1)} %get-tuple-element.183, s32[]{:T(128)} %get-tuple-element.170), kind=kOutput, calls=%fused_computation.1.clone.1 | convolution fusion | flops 304348416 | bytes 6098432 | tf_op jit(solution)/shard_map/while/body/eval_jaxpr/qhd,khd->hqk/dot_general | solution.py:75
  234.7 3.3 fusion.36
  238.0 0.5 copy-done
  238.4 2.5 fusion.38
  240.9 4.2 %bitcast_reduce_fusion.2 = (f32[3,256]{1,0:T(4,128)S(1)}, f32[3,1536,256]{2,1,0:T(8,128)}) fusion(bf16[256,3,128]{2,0,1:T(8,128)(2,1)S(1)} %get-tuple-element.184, bf16[8,1536,3,128]{3,1,2,0:T(8,128)(2,1)} %get-tuple-element.183, s32[]{:T(128)} %get-tuple-element.170), kind=kOutput, calls=%fused_computation.1.clone.1 | convolution fusion | flops 304348416 | bytes 6098432 | tf_op jit(solution)/shard_map/while/body/eval_jaxpr/qhd,khd->hqk/dot_general | solution.py:75
  245.2 3.3 fusion.36
  248.4 0.5 copy-done
  248.9 2.5 fusion.38
  251.4 4.2 %bitcast_reduce_fusion.2 = (f32[3,256]{1,0:T(4,128)S(1)}, f32[3,1536,256]{2,1,0:T(8,128)}) fusion(bf16[256,3,128]{2,0,1:T(8,128)(2,1)S(1)} %get-tuple-element.184, bf16[8,1536,3,128]{3,1,2,0:T(8,128)(2,1)} %get-tuple-element.183, s32[]{:T(128)} %get-tuple-element.170), kind=kOutput, calls=%fused_computation.1.clone.1 | convolution fusion | flops 304348416 | bytes 6098432 | tf_op jit(solution)/shard_map/while/body/eval_jaxpr/qhd,khd->hqk/dot_general | solution.py:75
  255.6 3.3 fusion.36
  258.9 0.5 copy-done
  259.4 2.5 fusion.38
  261.9 4.2 %bitcast_reduce_fusion.2 = (f32[3,256]{1,0:T(4,128)S(1)}, f32[3,1536,256]{2,1,0:T(8,128)}) fusion(bf16[256,3,128]{2,0,1:T(8,128)(2,1)S(1)} %get-tuple-element.184, bf16[8,1536,3,128]{3,1,2,0:T(8,128)(2,1)} %get-tuple-element.183, s32[]{:T(128)} %get-tuple-element.170), kind=kOutput, calls=%fused_computation.1.clone.1 | convolution fusion | flops 304348416 | bytes 6098432 | tf_op jit(solution)/shard_map/while/body/eval_jaxpr/qhd,khd->hqk/dot_general | solution.py:75
  266.1 3.3 fusion.36
  269.9 2.5 fusion.38
  272.4 4.2 %bitcast_reduce_fusion.2 = (f32[3,256]{1,0:T(4,128)S(1)}, f32[3,1536,256]{2,1,0:T(8,128)}) fusion(bf16[256,3,128]{2,0,1:T(8,128)(2,1)S(1)} %get-tuple-element.184, bf16[8,1536,3,128]{3,1,2,0:T(8,128)(2,1)} %get-tuple-element.183, s32[]{:T(128)} %get-tuple-element.170), kind=kOutput, calls=%fused_computation.1.clone.1 | convolution fusion | flops 304348416 | bytes 6098432 | tf_op jit(solution)/shard_map/while/body/eval_jaxpr/qhd,khd->hqk/dot_general | solution.py:75
  276.6 3.3 fusion.36
  279.9 0.5 copy-done
  280.4 2.5 fusion.38
  282.9 4.2 %bitcast_reduce_fusion.2 = (f32[3,256]{1,0:T(4,128)S(1)}, f32[3,1536,256]{2,1,0:T(8,128)}) fusion(bf16[256,3,128]{2,0,1:T(8,128)(2,1)S(1)} %get-tuple-element.184, bf16[8,1536,3,128]{3,1,2,0:T(8,128)(2,1)} %get-tuple-element.183, s32[]{:T(128)} %get-tuple-element.170), kind=kOutput, calls=%fused_computation.1.clone.1 | convolution fusion | flops 304348416 | bytes 6098432 | tf_op jit(solution)/shard_map/while/body/eval_jaxpr/qhd,khd->hqk/dot_general | solution.py:75
  287.1 3.3 fusion.36
  290.8 2.5 fusion.38
  293.4 4.2 %bitcast_reduce_fusion.2 = (f32[3,256]{1,0:T(4,128)S(1)}, f32[3,1536,256]{2,1,0:T(8,128)}) fusion(bf16[256,3,128]{2,0,1:T(8,128)(2,1)S(1)} %get-tuple-element.184, bf16[8,1536,3,128]{3,1,2,0:T(8,128)(2,1)} %get-tuple-element.183, s32[]{:T(128)} %get-tuple-element.170), kind=kOutput, calls=%fused_computation.1.clone.1 | convolution fusion | flops 304348416 | bytes 6098432 | tf_op jit(solution)/shard_map/while/body/eval_jaxpr/qhd,khd->hqk/dot_general | solution.py:75
  297.6 3.3 fusion.36
  300.9 0.5 copy-done
  301.3 2.5 fusion.38
  303.8 4.2 %bitcast_reduce_fusion.2 = (f32[3,256]{1,0:T(4,128)S(1)}, f32[3,1536,256]{2,1,0:T(8,128)}) fusion(bf16[256,3,128]{2,0,1:T(8,128)(2,1)S(1)} %get-tuple-element.184, bf16[8,1536,3,128]{3,1,2,0:T(8,128)(2,1)} %get-tuple-element.183, s32[]{:T(128)} %get-tuple-element.170), kind=kOutput, calls=%fused_computation.1.clone.1 | convolution fusion | flops 304348416 | bytes 6098432 | tf_op jit(solution)/shard_map/while/body/eval_jaxpr/qhd,khd->hqk/dot_general | solution.py:75
  308.1 3.3 fusion.36
  311.8 2.5 fusion.38
  314.5 3.7 convolution_convert_fusion
  318.2 2.6 copy.32
  320.8 84.5 %reduce-scatter.4.cloned.1.call-done = bf16[640,256]{1,0:T(8,128)(2,1)} async-done(((bf16[5120,256]{1,0:T(8,128)(2,1)}), bf16[640,256]{1,0:T(8,128)(2,1)}) %reduce-scatter.4.cloned.1.call-update) | async-done | bytes 327696
  405.2 1.9 copy.33
  (51 shorter events, 2.2 us)
Async XLA Ops:
  6.5 138.8 %all-gather.2.cloned.1.call-start = ((), (), s32[]{:S(2)}) async-start(), calls=%async_computation.2 | async-start | bytes 19464192 | tf_op jit(solution)/shard_map/all_gather | solution.py:38
  9.6 47.7 %copy-start.1 = (f32[5120]{0:T(1024)S(1)}, f32[5120]{0:T(1024)}, u32[]{:S(2)}) copy-start(f32[5120]{0:T(1024)} %param.9) | copy-start | bytes 61444
  11.3 45.3 %all-to-all-start = ((bf16[8,256,640]{1,2,0:T(8,128)(2,1)}), bf16[8,256,640]{1,2,0:T(8,128)(2,1)S(1)}, u32[]{:S(2)}, u32[]{:S(2)}) async-start(bf16[8,256,640]{1,2,0:T(8,128)(2,1)} %broadcast_in_dim.13), calls=%async_computation | async-start | bytes 5242880 | tf_op jit(solution)/shard_map/all_to_all | solution.py:16
  18.8 386.5 %reduce-scatter.4.cloned.1.call-start = ((), (), s32[]{:S(2)}) async-start(), calls=%async_computation.3 | async-start | bytes 2949120
  56.6 2.9 copy-start.2
  234.7 3.8 copy-start
  245.1 3.8 copy-start
  255.6 3.8 copy-start
  266.1 3.8 copy-start
  276.6 3.8 copy-start
  287.1 3.8 copy-start
  297.6 3.8 copy-start
  308.1 3.8 copy-start
Sparse Core Ops, SparseCore 0:
  9.2 136.0 all-gather.1
  320.9 84.2 reduce-scatter.3
where the time goes:
time: 416 us; the launch traced here: 414 us
  waiting for transfers between devices  206 us (50%)
  local copies, waits for them, and re-layouts  96.5 us (23%)
  matrix products  58.8 us (14%)
  other arithmetic  31.2 us (8%)
  between operations  13.5 us (3%)
  starting transfers between devices  7.51 us (2%)
    unnamed x3, waiting for transfers between devices  84.5 us
    all_gather x1, waiting for transfers between devices, in_one_piece(): lax.all_gather(both, axis, axis=dim, tiled=True)  83.9 us
    all_to_all x1, waiting for transfers between devices, sent_to_all(): lax.all_to_all(jnp.broadcast_to(array[None], (devices, *array.shape)), ax...  37.7 us
    dot_general x8, matrix products, step_block(): jnp.einsum('qhd,khd->hqk', query_heads, key_block, preferred_element_type...  33.7 us
    unnamed x10, local copies, waits for them, and re-layouts  27 us
    reduce_sum x8, other arithmetic, step_block(): new_sum = row_sum * factor + jnp.sum(exp_scores, axis=2)  26.2 us
    reshape x1, local copies, waits for them, and re-layouts, per_device(): key_rows.reshape(count // width_rows, width_rows, heads, HEAD_DIM)  24.5 us
    reshape x1, local copies, waits for them, and re-layouts, per_device(): value_rows.reshape(count // width_rows, width_rows, heads, HEAD_DIM)  24.5 us
  transfers between devices with their start and end apart: 3, of which 3 were waited for; matrix products, arithmetic and copies ran while one was open for 2% of the time, Pallas kernels for 0%

commit v1 on v0

v1 whole, which is shorter than its diff:
```python
import math

import jax
import jax.numpy as jnp
from jax import lax
from jax.experimental import pallas as pl
from jax.experimental.pallas import tpu as pltpu
from jax.sharding import PartitionSpec as P

HD = 128
NORM_EPS = 1e-06
MESH = pl.DeviceIdType.MESH
NZ, NX = 8, 4
F32, BF16 = jnp.float32, jnp.bfloat16
LOG2E = 1.4426950408889634


def body(x_hbm, gain_ref, wq_hbm, wo_hbm, k_hbm, v_hbm, out_ref,
         kbuf, vbuf, vtmp, xbuf, wq, wobuf, qacc, ssacc, qbuf, acc, mbuf, lbuf,
         osend, ssend, orecv, srecv, att, oacc,
         lsem, zss, zrs, bss, brs, xss, xrs, wss, wrs, wbs, wbr, qss, qrs,
         oss, ors, ass, ars):
    rows, xcols = x_hbm.shape
    toks = k_hbm.shape[0]
    heads = k_hbm.shape[1] // HD
    half = rows // 2
    blk, tp = lax.axis_index("blk"), lax.axis_index("tp")
    c = lax.rem(blk, 2)
    z = lax.rem(blk // 2, NZ)
    yl = blk // (2 * NZ)
    x, yh = tp // 2, lax.rem(tp, 2)

    def zdev(d):
        return ((yl * NZ + lax.rem(z + d + NZ, NZ)) * 2 + c, tp)

    def tpdev(dx, dy):
        return (blk, lax.rem(x + dx + NX, NX) * 2 + lax.rem(yh + dy, 2))

    def tpi(dx, dy):
        return lax.rem(x + dx + NX, NX) * 2 + lax.rem(yh + dy, 2)

    sib = (blk + 1 - 2 * c, tp)
    ypart = (blk + 2 * NZ - 4 * NZ * yl, tp)
    zsrc = lambda d: lax.rem(z + d + NZ, NZ)
    others = [(dx, dy) for dy in (0, 1) for dx in (0, 1, 3, 2) if (dx, dy) != (0, 0)]
    sends = []

    def rcopy(src, dst, ss, rs, dev):
        return pltpu.make_async_remote_copy(
            src_ref=src, dst_ref=dst, send_sem=ss, recv_sem=rs,
            device_id=dev, device_id_type=MESH)

    def send(src, dst, ss, rs, dev):
        cp = rcopy(src, dst, ss, rs, dev)
        cp.start()
        sends.append(cp)

    def await_recv(dst, ss, rs):
        rcopy(dst, dst, ss, rs, sib).wait_recv()

    def kslot(h, zz, cc):
        return kbuf.at[h, zz, pl.ds(cc * toks, toks), :]

    def vslot(h, zz, cc):
        return vbuf.at[h, zz, cc]

    kl = [pltpu.make_async_copy(k_hbm.at[:, pl.ds(h * HD, HD)], kslot(h, z, c), lsem.at[h]) for h in range(heads)]
    vl = [pltpu.make_async_copy(v_hbm.at[:, pl.ds(h * HD, HD)], vtmp.at[h], lsem.at[3 + h]) for h in range(heads)]
    xl = pltpu.make_async_copy(x_hbm, xbuf.at[tp], lsem.at[6])
    wql = pltpu.make_async_copy(wq_hbm, wq, lsem.at[7])
    wol = pltpu.make_async_copy(wo_hbm.at[:, :, pl.ds(pl.multiple_of(tp * xcols, HD), xcols)], wobuf.at[:, tp], lsem.at[8])
    kl[0].start()
    vl[0].start()
    xl.start()
    for h in range(1, heads):
        kl[h].start()
        vl[h].start()
    wql.start()
    wol.start()

    bar = pltpu.get_barrier_semaphore()
    peers = [zdev(1), zdev(-1), sib, ypart] + [tpdev(dx, dy) for dx, dy in others]
    for dev in peers:
        pl.semaphore_signal(bar, inc=1, device_id=dev, device_id_type=MESH)
    pl.semaphore_wait(bar, len(peers))

    def zsend(h, s, d, kv):
        src_z = zsrc(-s if d == 0 else s)
        ref = kslot(h, src_z, c) if kv == 0 else vslot(h, src_z, c)
        send(ref, ref, zss.at[d, s, h, kv], zrs.at[d, s, h, kv], zdev(1 if d == 0 else -1))

    def bsend(h, src_z, slot, kv):
        ref = kslot(h, src_z, c) if kv == 0 else vslot(h, src_z, c)
        send(ref, ref, bss.at[slot, h, kv], brs.at[slot, h, kv], sib)

    def own(h):
        kl[h].wait()
        zsend(h, 0, 0, 0)
        vl[h].wait()
        vbuf[h, z, c] = vtmp[h].T
        zsend(h, 0, 1, 1)
        zsend(h, 0, 0, 1)
        zsend(h, 0, 1, 0)
        bsend(h, z, 0, 0)
        bsend(h, z, 0, 1)

    def slot_of(d, s):
        return 2 * s - 1 + d if s < 4 else 7

    def arrive(h, s):
        order = [(0, 0), (1, 1), (0, 1), (1, 0)]
        for d, kv in order:
            if s == 4 and kv != d:
                continue
            src_z = zsrc(-s if d == 0 else s)
            ref = kslot(h, src_z, c) if kv == 0 else vslot(h, src_z, c)
            await_recv(ref, zss.at[d, s - 1, h, kv], zrs.at[d, s - 1, h, kv])
            if s < 3 or (s == 3 and kv == d):
                zsend(h, s, d, kv)
            bsend(h, src_z, slot_of(d, s), kv)

    def sib_arrive(h, s):
        if s == 0:
            lst = [(z, 0)]
        elif s == 4:
            lst = [(zsrc(4), 7)]
        else:
            lst = [(zsrc(-s), slot_of(0, s)), (zsrc(s), slot_of(1, s))]
        for src_z, slot in lst:
            await_recv(kslot(h, src_z, 1 - c), bss.at[slot, h, 0], brs.at[slot, h, 0])
            await_recv(vslot(h, src_z, 1 - c), bss.at[slot, h, 1], brs.at[slot, h, 1])

    XOWN_R, XOWN_L, XY, XP_R, XP_L, XOH_R, XOH_L, XPH_R, XPH_L = range(9)

    def xsend(ref, i, dx, dy):
        send(ref, ref, xss.at[i], xrs.at[i], tpdev(dx, dy))

    def xwait(ref, i):
        await_recv(ref, xss.at[i], xrs.at[i])

    def xfull(t):
        return xbuf.at[t]

    def xtop(t):
        return xbuf.at[t, pl.ds(0, half), :]

    def xbot(t):
        return xbuf.at[t, pl.ds(half, half), :]

    def qblock(t, first=False):
        xf = xbuf[t].astype(F32)
        sq = xf * xf
        part = sq[:, 0:HD]
        for j in range(1, xcols // HD):
            part = part + sq[:, j * HD:(j + 1) * HD]
        g = gain_ref[:, pl.ds(pl.multiple_of(t * xcols, HD), xcols)]
        xg = (xf * g).astype(BF16)
        prod = jnp.dot(xg, wq[t], preferred_element_type=F32)
        if first:
            ssacc[...] = part
            qacc[...] = prod
        else:
            ssacc[...] += part
            qacc[...] += prod

    def init_state():
        mbuf[...] = jnp.full(mbuf.shape, -1e30, F32)
        lbuf[...] = jnp.zeros(lbuf.shape, F32)
        acc[...] = jnp.zeros(acc.shape, F32)

    def tile(h, zz, r):
        s = lax.dot_general(kbuf[h, zz], qbuf[h, r], (((1,), (1,)), ((), ())), preferred_element_type=F32)
        mo = mbuf[h, r]
        mn = jnp.maximum(mo, jnp.max(s, axis=0, keepdims=True))
        p = jnp.exp2(s - mn)
        f = jnp.exp2(mo - mn)
        lbuf[h, r] = lbuf[h, r] * f + jnp.sum(p, axis=0, keepdims=True)
        vv = jnp.concatenate([vbuf[h, zz, 0], vbuf[h, zz, 1]], axis=1)
        o = jnp.dot(vv, p.astype(BF16), preferred_element_type=F32)
        acc[h, r] = acc[h, r] * f + o
        mbuf[h, r] = mn

    def tiles(h, z0, n, stride, r0, nr):
        def step(i, carry):
            tile(h, zsrc(z0 + stride * (i // nr)), r0 + lax.rem(i, nr))
            return carry
        lax.fori_loop(0, n * nr, step, 0)

    def finish_partner(h):
        osend[h] = acc[h, 1].astype(BF16)
        ssend[h, 0:1] = mbuf[h, 1]
        ssend[h, 1:2] = lbuf[h, 1]
        send(osend.at[h], orecv.at[h], oss.at[h, 0], ors.at[h, 0], ypart)
        send(ssend.at[h], srecv.at[h], oss.at[h, 1], ors.at[h, 1], ypart)

    def merge(h):
        await_recv(orecv.at[h], oss.at[h, 0], ors.at[h, 0])
        await_recv(srecv.at[h], oss.at[h, 1], ors.at[h, 1])
        ma, mb = mbuf[h, 0], srecv[h, 0:1]
        m = jnp.maximum(ma, mb)
        fa, fb = jnp.exp2(ma - m), jnp.exp2(mb - m)
        tot = lbuf[h, 0] * fa + srecv[h, 1:2] * fb
        o = (acc[h, 0] * fa + orecv[h].astype(F32) * fb) / tot
        att[h, tp] = o.T.astype(BF16)
        for i, (dx, dy) in enumerate(others):
            send(att.at[h, tp], att.at[h, tp], ass.at[h, i], ars.at[h, i], tpdev(dx, dy))

    def out_part(h, first=False):
        for i, (dx, dy) in enumerate(others):
            t = tpi(-dx, dy)
            await_recv(att.at[h, t], ass.at[h, i], ars.at[h, i])
        a = jnp.concatenate([att[h, t] for t in range(8)], axis=1)
        w = wobuf[h].reshape(8 * HD, xcols)
        prod = jnp.dot(a, w, preferred_element_type=F32)
        if first:
            oacc[...] = prod
        else:
            oacc[...] += prod

    hh = HD // 2

    def wslot(t, cc):
        return wobuf.at[:, t, pl.ds(cc * hh, hh), :]

    def wsend():
        for i, (dx, dy) in enumerate(others):
            t = tpi(dx, dy)
            src = wo_hbm.at[:, pl.ds(c * hh, hh), pl.ds(pl.multiple_of(t * xcols, HD), xcols)]
            send(src, wslot(tp, c), wss.at[i], wrs.at[i], tpdev(dx, dy))

    def wfwd():
        for i, (dx, dy) in enumerate(others):
            t = tpi(-dx, dy)
            await_recv(wslot(t, c), wss.at[i], wrs.at[i])
            send(wslot(t, c), wslot(t, c), wbs.at[i], wbr.at[i], sib)

    def wdone():
        wol.wait()
        for i, (dx, dy) in enumerate(others):
            t = tpi(-dx, dy)
            await_recv(wslot(t, 1 - c), wbs.at[i], wbr.at[i])

    tl, tr, t2 = tpi(-1, 0), tpi(1, 0), tpi(2, 0)
    pt, ptl, ptr, pt2 = tpi(0, 1), tpi(-1, 1), tpi(1, 1), tpi(2, 1)

    own(0)
    xl.wait()
    xsend(xfull(tp), XOWN_R, 1, 0)
    xsend(xfull(tp), XOWN_L, -1, 0)
    xsend(xfull(tp), XY, 0, 1)
    own(1)
    init_state()
    wql.wait()
    qblock(tp, True)
    arrive(0, 1)
    own(2)
    xwait(xfull(tl), XOWN_R)
    xsend(xtop(tl), XOH_R, 1, 0)
    xwait(xfull(tr), XOWN_L)
    xsend(xbot(tr), XOH_L, -1, 0)
    xwait(xfull(pt), XY)
    xsend(xfull(pt), XP_R, 1, 0)
    xsend(xfull(pt), XP_L, -1, 0)
    qblock(tl)
    qblock(tr)
    qblock(pt)
    arrive(0, 2)
    xwait(xtop(t2), XOH_R)
    xwait(xbot(t2), XOH_L)
    qblock(t2)
    arrive(1, 1)
    xwait(xfull(ptl), XP_R)
    xsend(xtop(ptl), XPH_R, 1, 0)
    xwait(xfull(ptr), XP_L)
    xsend(xbot(ptr), XPH_L, -1, 0)
    wsend()
    qblock(ptl)
    qblock(ptr)
    arrive(0, 3)
    arrive(1, 2)
    xwait(xtop(pt2), XPH_R)
    xwait(xbot(pt2), XPH_L)
    qblock(pt2)

    mean_sq = jnp.sum(ssacc[...], axis=1, keepdims=True) * (1.0 / (8 * xcols))
    scale = lax.rsqrt(mean_sq + NORM_EPS) * (LOG2E / math.sqrt(HD))
    for h in range(heads):
        qbuf[h, 0] = (qacc[:, h * HD:(h + 1) * HD] * scale).astype(BF16)
        send(qbuf.at[h, 0], qbuf.at[h, 1], qss.at[h], qrs.at[h], ypart)

    def qwait(h):
        await_recv(qbuf.at[h, 1], qss.at[h], qrs.at[h])

    arrive(0, 4)
    for s in range(5):
        sib_arrive(0, s)
    tiles(0, 0, 8, 1, 0, 1)
    arrive(2, 1)
    for s in range(2):
        sib_arrive(1, s)
        sib_arrive(2, s)
    tiles(1, -1, 3, 1, 0, 1)
    qwait(0)
    tiles(0, 0, 8, 1, 1, 1)
    finish_partner(0)
    arrive(1, 3)
    tiles(2, -1, 3, 1, 0, 1)
    qwait(1)
    tiles(1, -1, 3, 1, 1, 1)
    merge(0)
    arrive(2, 2)
    sib_arrive(1, 2)
    tiles(1, -2, 2, 4, 0, 2)
    qwait(2)
    tiles(2, -1, 3, 1, 1, 1)
    arrive(1, 4)
    sib_arrive(1, 3)
    sib_arrive(1, 4)
    tiles(1, 3, 3, 1, 0, 2)
    arrive(2, 3)
    finish_partner(1)
    sib_arrive(2, 2)
    tiles(2, -2, 2, 4, 0, 2)
    merge(1)
    arrive(2, 4)
    sib_arrive(2, 3)
    tiles(2, -3, 2, 6, 0, 2)
    sib_arrive(2, 4)
    tiles(2, 4, 1, 1, 0, 2)
    finish_partner(2)
    wfwd()
    merge(2)
    wdone()
    out_part(0, True)
    out_part(1)
    out_part(2)
    out_ref[...] = oacc[...].astype(BF16)
    for cp in sends:
        cp.wait_send()


def per_device(dec_states, norm_gain, query_weight, out_weight, enc_keys, enc_values):
    rows, xcols = dec_states.shape
    toks, width = enc_keys.shape
    heads = width // HD
    vm = pltpu.VMEM
    dma = pltpu.SemaphoreType.DMA
    hbm = pl.BlockSpec(memory_space=pl.ANY)
    inv = pl.BlockSpec(memory_space=pltpu.VMEM)
    return pl.pallas_call(
        body,
        out_shape=jax.ShapeDtypeStruct((rows, xcols), BF16),
        in_specs=[hbm, inv, hbm, hbm, hbm, hbm],
        out_specs=inv,
        scratch_shapes=[
            vm((heads, NZ, 2 * toks, HD), BF16),
            vm((heads, NZ, 2, HD, toks), BF16),
            vm((heads, toks, HD), BF16),
            vm((8, rows, xcols), BF16),
            vm((8, xcols, width), BF16),
            vm((heads, 8, HD, xcols), BF16),
            vm((rows, width), F32),
            vm((rows, HD), F32),
            vm((heads, 2, rows, HD), BF16),
            vm((heads, 2, HD, rows), F32),
            vm((heads, 2, 1, rows), F32),
            vm((heads, 2, 1, rows), F32),
            vm((heads, HD, rows), BF16),
            vm((heads, 8, rows), F32),
            vm((heads, HD, rows), BF16),
            vm((heads, 8, rows), F32),
            vm((heads, 8, rows, HD), BF16),
            vm((rows, xcols), F32),
            dma((9,)),
            dma((2, 4, heads, 2)), dma((2, 4, heads, 2)),
            dma((8, heads, 2)), dma((8, heads, 2)),
            dma((9,)), dma((9,)),
            dma((7,)), dma((7,)),
            dma((7,)), dma((7,)),
            dma((heads,)), dma((heads,)),
            dma((heads, 2)), dma((heads, 2)),
            dma((heads, 7)), dma((heads, 7)),
        ],
        compiler_params=pltpu.CompilerParams(
            collective_id=0, has_side_effects=True, vmem_limit_bytes=60 * 2**20),
    )(
        dec_states,
        norm_gain.reshape(1, -1),
        query_weight.reshape(8, xcols, width),
        out_weight.reshape(heads, HD, 8 * xcols),
        enc_keys,
        enc_values,
    )


def solution(mesh):
    in_specs = (P("blk", "tp"), P(), P(None, "tp"), P("tp", None), P("blk", "tp"), P("blk", "tp"))
    return jax.shard_map(
        per_device, mesh=mesh, in_specs=in_specs, out_specs=P("blk", "tp"), check_vma=False
    )
```

time: 416 us -> 105 us (0.25)
  the two profiles are of different devices: /device:TPU:1 before, /device:TPU:23 now
where the time goes in v1:
time: 105 us
  Pallas kernels  103 us (98%)
  local copies, waits for them, and re-layouts  1.73 us (2%)
    pallas_call x1, Pallas kernels, per_device(): pl.pallas_call(body, out_shape=jax.ShapeDtypeStruct((rows, xcols), BF16),...  103 us

profile of v1, /device:TPU:23, one launch (start us, length us, event | category | flops | bytes accessed | tf_op | source)
XLA Modules:
  0.0 105.1 jit_solution(316932848739534149)
XLA Ops:
  0.0 103.3 %shard_map.64 = bf16[256,640]{1,0:T(8,128)(2,1)} custom-call(bf16[256,640]{1,0:T(8,128)(2,1)} %x_hbm.1, f32[1,5120]{1,0:T(1,128)} %bitcast.5, bf16[8,640,384]{2,1,0:T(8,128)(2,1)} %bitcast.3, bf16[3,128,5120]{2,1,0:T(8,128)(2,1)} %bitcast.4, bf16[384,384]{1,0:T(8,128)(2,1)} %k_hbm.1, bf16[384,384]{1,0:T(8,128)(2,1)} %v_hbm.1), custom_call_target="tpu_custom_call" | custom-call | tf_op jit(solution)/shard_map/pallas_call | solution.py:350
  103.3 1.7 %copy.8 = bf16[256,640]{1,0:T(8,128)(2,1)} copy(bf16[256,640]{1,0:T(8,128)(2,1)} %shard_map.64) | data formatting | bytes 655360

commit v2 on v1

--- a/solution.py
+++ b/solution.py
@@ -17,8 +17,8 @@
 
 def body(x_hbm, gain_ref, wq_hbm, wo_hbm, k_hbm, v_hbm, out_ref,
          kbuf, vbuf, vtmp, xbuf, wq, wobuf, qacc, ssacc, qbuf, acc, mbuf, lbuf,
-         osend, ssend, orecv, srecv, att, oacc,
-         lsem, zss, zrs, bss, brs, xss, xrs, wss, wrs, wbs, wbr, qss, qrs,
+         osend, ssend, orecv, srecv, att, oacc, wst,
+         sbuf, lsem, zss, zrs, bss, brs, xss, xrs, wss, wrs, wbs, wbr, wys, wyr, qss, qrs,
          oss, ors, ass, ars):
     rows, xcols = x_hbm.shape
     toks = k_hbm.shape[0]
@@ -42,7 +42,7 @@
     sib = (blk + 1 - 2 * c, tp)
     ypart = (blk + 2 * NZ - 4 * NZ * yl, tp)
     zsrc = lambda d: lax.rem(z + d + NZ, NZ)
-    others = [(dx, dy) for dy in (0, 1) for dx in (0, 1, 3, 2) if (dx, dy) != (0, 0)]
+    DX = (1, 3, 2)
     sends = []
 
     def rcopy(src, dst, ss, rs, dev):
@@ -79,7 +79,7 @@
     wol.start()
 
     bar = pltpu.get_barrier_semaphore()
-    peers = [zdev(1), zdev(-1), sib, ypart] + [tpdev(dx, dy) for dx, dy in others]
+    peers = [zdev(1), zdev(-1), sib, ypart, tpdev(0, 1)] + [tpdev(dx, 0) for dx in DX]
     for dev in peers:
         pl.semaphore_signal(bar, inc=1, device_id=dev, device_id_type=MESH)
     pl.semaphore_wait(bar, len(peers))
@@ -168,23 +168,48 @@
         lbuf[...] = jnp.zeros(lbuf.shape, F32)
         acc[...] = jnp.zeros(acc.shape, F32)
 
-    def tile(h, zz, r):
-        s = lax.dot_general(kbuf[h, zz], qbuf[h, r], (((1,), (1,)), ((), ())), preferred_element_type=F32)
+    def update(h, r, s, vv):
         mo = mbuf[h, r]
         mn = jnp.maximum(mo, jnp.max(s, axis=0, keepdims=True))
-        p = jnp.exp2(s - mn)
+        p = jnp.exp2(s - mn).astype(BF16)
         f = jnp.exp2(mo - mn)
-        lbuf[h, r] = lbuf[h, r] * f + jnp.sum(p, axis=0, keepdims=True)
-        vv = jnp.concatenate([vbuf[h, zz, 0], vbuf[h, zz, 1]], axis=1)
-        o = jnp.dot(vv, p.astype(BF16), preferred_element_type=F32)
-        acc[h, r] = acc[h, r] * f + o
+        ones = jnp.ones((16, vv.shape[1]), BF16)
+        o = jnp.dot(jnp.concatenate([vv, ones], axis=0), p, preferred_element_type=F32)
+        lbuf[h, r] = lbuf[h, r] * f + o[HD:HD + 1]
+        acc[h, r] = acc[h, r] * f + o[:HD]
         mbuf[h, r] = mn
 
-    def tiles(h, z0, n, stride, r0, nr):
-        def step(i, carry):
-            tile(h, zsrc(z0 + stride * (i // nr)), r0 + lax.rem(i, nr))
-            return carry
-        lax.fori_loop(0, n * nr, step, 0)
+    cur = []
+
+    def feed(h, d):
+        zz = zsrc(d)
+        par = (cur[0][2] + 1) % 2 if cur else 0
+        old = cur.pop() if cur else None
+        vv = None if old is None else values(old[0], old[1])
+        for r in range(2):
+            sbuf[2 * par + r] = scores(h, zz, r)
+            if old is not None:
+                update(old[0], r, sbuf[2 * old[2] + r], vv)
+        cur.append((h, zz, par))
+
+    def flush():
+        h, zz, par = cur.pop()
+        vv = values(h, zz)
+        for r in range(2):
+            update(h, r, sbuf[2 * par + r], vv)
+
+    def flush_last():
+        h, zz, par = cur.pop()
+        vv = values(h, zz)
+        update(h, 1, sbuf[2 * par + 1], vv)
+        finish_partner(h)
+        update(h, 0, sbuf[2 * par], vv)
+
+    def scores(h, zz, r):
+        return lax.dot_general(kbuf[h, zz], qbuf[h, r], (((1,), (1,)), ((), ())), preferred_element_type=F32)
+
+    def values(h, zz):
+        return jnp.concatenate([vbuf[h, zz, 0], vbuf[h, zz, 1]], axis=1)
 
     def finish_partner(h):
         osend[h] = acc[h, 1].astype(BF16)
@@ -202,13 +227,28 @@
         tot = lbuf[h, 0] * fa + srecv[h, 1:2] * fb
         o = (acc[h, 0] * fa + orecv[h].astype(F32) * fb) / tot
         att[h, tp] = o.T.astype(BF16)
-        for i, (dx, dy) in enumerate(others):
-            send(att.at[h, tp], att.at[h, tp], ass.at[h, i], ars.at[h, i], tpdev(dx, dy))
+        att_send(h, tp, 0)
+        att_one(h, tp, 3, 0, 1)
+
+    def att_one(h, t, i, dx, dy):
+        send(att.at[h, t], att.at[h, t], ass.at[h, i], ars.at[h, i], tpdev(dx, dy))
+
+    def att_send(h, t, base):
+        for i, dx in enumerate(DX):
+            att_one(h, t, base + i, dx, 0)
+
+    def att_wait(h, i, dx, dy):
+        await_recv(att.at[h, tpi(-dx, dy)], ass.at[h, i], ars.at[h, i])
+
+    def att_relay(h):
+        att_wait(h, 3, 0, 1)
+        att_send(h, tpi(0, 1), 4)
 
     def out_part(h, first=False):
-        for i, (dx, dy) in enumerate(others):
-            t = tpi(-dx, dy)
-            await_recv(att.at[h, t], ass.at[h, i], ars.at[h, i])
+        for i, dx in enumerate(DX):
+            att_wait(h, i, dx, 0)
+        for i, dx in enumerate(DX):
+            att_wait(h, 4 + i, dx, 1)
         a = jnp.concatenate([att[h, t] for t in range(8)], axis=1)
         w = wobuf[h].reshape(8 * HD, xcols)
         prod = jnp.dot(a, w, preferred_element_type=F32)
@@ -217,29 +257,49 @@
         else:
             oacc[...] += prod
 
-    hh = HD // 2
-
-    def wslot(t, cc):
-        return wobuf.at[:, t, pl.ds(cc * hh, hh), :]
-
-    def wsend():
-        for i, (dx, dy) in enumerate(others):
-            t = tpi(dx, dy)
-            src = wo_hbm.at[:, pl.ds(c * hh, hh), pl.ds(pl.multiple_of(t * xcols, HD), xcols)]
-            send(src, wslot(tp, c), wss.at[i], wrs.at[i], tpdev(dx, dy))
-
-    def wfwd():
-        for i, (dx, dy) in enumerate(others):
-            t = tpi(-dx, dy)
-            await_recv(wslot(t, c), wss.at[i], wrs.at[i])
-            send(wslot(t, c), wslot(t, c), wbs.at[i], wbr.at[i], sib)
+    hh = HD // 4
+
+    def wslot(t, cc, yy):
+        return wobuf.at[:, t, pl.ds((2 * cc + yy) * hh, hh), :]
+
+    def wsrc(t):
+        return wo_hbm.at[:, pl.ds((2 * c + yl) * hh, hh), pl.ds(pl.multiple_of(t * xcols, HD), xcols)]
+
+    def w_own(i):
+        send(wsrc(tpi(DX[i], 0)), wslot(tp, c, yl), wss.at[i], wrs.at[i], tpdev(DX[i], 0))
+
+    def w_y():
+        for i, dx in enumerate(DX):
+            send(wsrc(tpi(dx, 1)), wst.at[i], wss.at[7 + i], wrs.at[7 + i], tpdev(0, 1))
+        send(wsrc(tpi(0, 1)), wslot(tp, c, yl), wss.at[6], wrs.at[6], tpdev(0, 1))
+
+    def w_relay(i):
+        await_recv(wst.at[i], wss.at[7 + i], wrs.at[7 + i])
+        send(wst.at[i], wslot(tpi(0, 1), c, yl), wss.at[3 + i], wrs.at[3 + i], tpdev(DX[i], 0))
+
+    def w_from(i):
+        return tpi(0, 1) if i == 6 else tpi(-DX[i % 3], i // 3)
+
+    def wfwd(i):
+        ref = wslot(w_from(i), c, yl)
+        await_recv(ref, wss.at[i], wrs.at[i])
+        send(ref, ref, wys.at[i], wyr.at[i], ypart)
+        send(ref, ref, wbs.at[0, i], wbr.at[0, i], sib)
+
+    def wfwd2():
+        for i in W_ORDER:
+            ref = wslot(w_from(i), c, 1 - yl)
+            await_recv(ref, wys.at[i], wyr.at[i])
+            send(ref, ref, wbs.at[1, i], wbr.at[1, i], sib)
 
     def wdone():
         wol.wait()
-        for i, (dx, dy) in enumerate(others):
-            t = tpi(-dx, dy)
-            await_recv(wslot(t, 1 - c), wbs.at[i], wbr.at[i])
-
+        for j in range(2):
+            for i in W_ORDER:
+                ref = wslot(w_from(i), 1 - c, yl if j == 0 else 1 - yl)
+                await_recv(ref, wbs.at[j, i], wbr.at[j, i])
+
+    W_ORDER = (0, 1, 6, 2, 3, 4, 5)
     tl, tr, t2 = tpi(-1, 0), tpi(1, 0), tpi(2, 0)
     pt, ptl, ptr, pt2 = tpi(0, 1), tpi(-1, 1), tpi(1, 1), tpi(2, 1)
 
@@ -249,6 +309,9 @@
     xsend(xfull(tp), XOWN_L, -1, 0)
     xsend(xfull(tp), XY, 0, 1)
     own(1)
+    w_y()
+    w_own(0)
+    w_own(1)
     init_state()
     wql.wait()
     qblock(tp, True)
@@ -265,19 +328,26 @@
     qblock(tr)
     qblock(pt)
     arrive(0, 2)
+    arrive(1, 1)
     xwait(xtop(t2), XOH_R)
     xwait(xbot(t2), XOH_L)
     qblock(t2)
-    arrive(1, 1)
+    wfwd(0)
+    wfwd(1)
     xwait(xfull(ptl), XP_R)
     xsend(xtop(ptl), XPH_R, 1, 0)
     xwait(xfull(ptr), XP_L)
     xsend(xbot(ptr), XPH_L, -1, 0)
-    wsend()
+    w_own(2)
     qblock(ptl)
     qblock(ptr)
     arrive(0, 3)
+    w_relay(0)
+    w_relay(1)
+    w_relay(2)
+    wfwd(6)
     arrive(1, 2)
+    arrive(2, 1)
     xwait(xtop(pt2), XPH_R)
     xwait(xbot(pt2), XPH_L)
     qblock(pt2)
@@ -292,44 +362,65 @@
         await_recv(qbuf.at[h, 1], qss.at[h], qrs.at[h])
 
     arrive(0, 4)
-    for s in range(5):
-        sib_arrive(0, s)
-    tiles(0, 0, 8, 1, 0, 1)
-    arrive(2, 1)
-    for s in range(2):
-        sib_arrive(1, s)
-        sib_arrive(2, s)
-    tiles(1, -1, 3, 1, 0, 1)
+    for st in range(5):
+        sib_arrive(0, st)
     qwait(0)
-    tiles(0, 0, 8, 1, 1, 1)
+    feed(0, 0)
+    feed(0, -1)
+    feed(0, 1)
+    arrive(1, 3)
+    wfwd(3)
+    feed(0, -2)
+    feed(0, 2)
+    feed(0, -3)
+    wfwd(2)
+    feed(0, 3)
+    feed(0, 4)
+    sib_arrive(1, 0)
+    sib_arrive(1, 1)
+    qwait(1)
+    feed(1, 0)
     finish_partner(0)
-    arrive(1, 3)
-    tiles(2, -1, 3, 1, 0, 1)
-    qwait(1)
-    tiles(1, -1, 3, 1, 1, 1)
-    merge(0)
     arrive(2, 2)
+    feed(1, -1)
+    feed(1, 1)
     sib_arrive(1, 2)
-    tiles(1, -2, 2, 4, 0, 2)
-    qwait(2)
-    tiles(2, -1, 3, 1, 1, 1)
+    feed(1, -2)
+    feed(1, 2)
     arrive(1, 4)
     sib_arrive(1, 3)
+    feed(1, -3)
+    feed(1, 3)
     sib_arrive(1, 4)
-    tiles(1, 3, 3, 1, 0, 2)
+    feed(1, 4)
+    qwait(2)
+    sib_arrive(2, 0)
+    sib_arrive(2, 1)
+    feed(2, 0)
+    finish_partner(1)
+    merge(0)
     arrive(2, 3)
-    finish_partner(1)
+    feed(2, -1)
+    feed(2, 1)
+    wfwd(4)
     sib_arrive(2, 2)
-    tiles(2, -2, 2, 4, 0, 2)
+    feed(2, -2)
+    feed(2, 2)
+    sib_arrive(2, 3)
+    feed(2, -3)
+    feed(2, 3)
     merge(1)
+    flush()
+    att_relay(0)
+    wfwd(5)
     arrive(2, 4)
-    sib_arrive(2, 3)
-    tiles(2, -3, 2, 6, 0, 2)
     sib_arrive(2, 4)
-    tiles(2, 4, 1, 1, 0, 2)
-    finish_partner(2)
-    wfwd()
+    feed(2, 4)
+    flush_last()
+    att_relay(1)
+    wfwd2()
     merge(2)
+    att_relay(2)
     wdone()
     out_part(0, True)
     out_part(1)
@@ -345,11 +436,11 @@
     heads = width // HD
     vm = pltpu.VMEM
     dma = pltpu.SemaphoreType.DMA
-    hbm = pl.BlockSpec(memory_space=pl.ANY)
+    hbm = pl.BlockSpec(memory_space=pltpu.HBM)
     inv = pl.BlockSpec(memory_space=pltpu.VMEM)
     return pl.pallas_call(
         body,
-        out_shape=jax.ShapeDtypeStruct((rows, xcols), BF16),
+        out_shape=pltpu.VMEM((rows, xcols), BF16),
         in_specs=[hbm, inv, hbm, hbm, hbm, hbm],
         out_specs=inv,
         scratch_shapes=[
@@ -371,11 +462,14 @@
             vm((heads, 8, rows), F32),
             vm((heads, 8, rows, HD), BF16),
             vm((rows, xcols), F32),
+            vm((3, heads, HD // 4, xcols), BF16),
+            vm((4, 2 * toks, rows), F32),
             dma((9,)),
             dma((2, 4, heads, 2)), dma((2, 4, heads, 2)),
             dma((8, heads, 2)), dma((8, heads, 2)),
             dma((9,)), dma((9,)),
-            dma((7,)), dma((7,)),
+            dma((10,)), dma((10,)),
+            dma((2, 7)), dma((2, 7)),
             dma((7,)), dma((7,)),
             dma((heads,)), dma((heads,)),
             dma((heads, 2)), dma((heads, 2)),

time: 105 us -> 80.1 us (0.76)
  the two profiles are of different devices: /device:TPU:23 before, /device:TPU:1 now
where the time goes in v2:
time: 80.1 us; the launch traced here: 79.2 us
  Pallas kernels  78.5 us (98%)
    pallas_call x1, Pallas kernels, per_device(): pl.pallas_call(body, out_shape=pltpu.VMEM((rows, xcols), BF16), in_specs=...  78.5 us

profile of v2, /device:TPU:1, one launch (start us, length us, event | category | flops | bytes accessed | tf_op | source)
XLA Modules:
  0.0 79.2 jit_solution(15485005919400517233)
XLA Ops:
  0.0 78.5 %shard_map.64 = bf16[256,640]{1,0:T(8,128)(2,1)S(1)} custom-call(bf16[256,640]{1,0:T(8,128)(2,1)} %x_hbm.1, f32[1,5120]{1,0:T(1,128)} %bitcast.5, bf16[8,640,384]{2,1,0:T(8,128)(2,1)} %bitcast.3, bf16[3,128,5120]{2,1,0:T(8,128)(2,1)} %bitcast.4, bf16[384,384]{1,0:T(8,128)(2,1)} %k_hbm.1, bf16[384,384]{1,0:T(8,128)(2,1)} %v_hbm.1), custom_call_target="tpu_custom_call" | custom-call | tf_op jit(solution)/shard_map/pallas_call | solution.py:441
  78.5 0.7 copy.8

commit v3 on v2

--- a/solution.py
+++ b/solution.py
@@ -107,8 +107,9 @@
     def slot_of(d, s):
         return 2 * s - 1 + d if s < 4 else 7
 
-    def arrive(h, s):
-        order = [(0, 0), (1, 1), (0, 1), (1, 0)]
+    ALL = ((0, 0), (1, 1), (0, 1), (1, 0))
+
+    def arrive(h, s, order=ALL):
         for d, kv in order:
             if s == 4 and kv != d:
                 continue
@@ -181,29 +182,32 @@
 
     cur = []
 
+    def stream(items):
+        par = (cur[0][1] + 1) % 2 if cur else 0
+        old, old_par = cur.pop() if cur else ((), 0)
+        for i in range(2):
+            if items:
+                h, d, r = items[i]
+                sbuf[2 * par + i] = scores(h, zsrc(d), r)
+            if old:
+                h, d, r = old[i]
+                update(h, r, sbuf[2 * old_par + i], values(h, zsrc(d)))
+        if items:
+            cur.append((items, par))
+
     def feed(h, d):
-        zz = zsrc(d)
-        par = (cur[0][2] + 1) % 2 if cur else 0
-        old = cur.pop() if cur else None
-        vv = None if old is None else values(old[0], old[1])
-        for r in range(2):
-            sbuf[2 * par + r] = scores(h, zz, r)
-            if old is not None:
-                update(old[0], r, sbuf[2 * old[2] + r], vv)
-        cur.append((h, zz, par))
-
-    def flush():
-        h, zz, par = cur.pop()
-        vv = values(h, zz)
-        for r in range(2):
-            update(h, r, sbuf[2 * par + r], vv)
+        stream(((h, d, 1), (h, d, 0)))
+
+    def feed_rows(h, r, d0, d1):
+        stream(((h, d0, r), (h, d1, r)))
 
     def flush_last():
-        h, zz, par = cur.pop()
-        vv = values(h, zz)
-        update(h, 1, sbuf[2 * par + 1], vv)
-        finish_partner(h)
-        update(h, 0, sbuf[2 * par], vv)
+        old, par = cur.pop()
+        for i in range(2):
+            h, d, r = old[i]
+            update(h, r, sbuf[2 * par + i], values(h, zsrc(d)))
+            if i == 0:
+                finish_partner(h)
 
     def scores(h, zz, r):
         return lax.dot_general(kbuf[h, zz], qbuf[h, r], (((1,), (1,)), ((), ())), preferred_element_type=F32)
@@ -227,15 +231,15 @@
         tot = lbuf[h, 0] * fa + srecv[h, 1:2] * fb
         o = (acc[h, 0] * fa + orecv[h].astype(F32) * fb) / tot
         att[h, tp] = o.T.astype(BF16)
+        att_one(h, tp, 3, 0, 1)
         att_send(h, tp, 0)
-        att_one(h, tp, 3, 0, 1)
 
     def att_one(h, t, i, dx, dy):
         send(att.at[h, t], att.at[h, t], ass.at[h, i], ars.at[h, i], tpdev(dx, dy))
 
     def att_send(h, t, base):
-        for i, dx in enumerate(DX):
-            att_one(h, t, base + i, dx, 0)
+        for i in (2, 0, 1):
+            att_one(h, t, base + i, DX[i], 0)
 
     def att_wait(h, i, dx, dy):
         await_recv(att.at[h, tpi(-dx, dy)], ass.at[h, i], ars.at[h, i])
@@ -361,65 +365,68 @@
     def qwait(h):
         await_recv(qbuf.at[h, 1], qss.at[h], qrs.at[h])
 
+    sib_arrive(0, 0)
+    sib_arrive(0, 1)
+    sib_arrive(0, 2)
+    feed_rows(0, 0, 0, -1)
     arrive(0, 4)
-    for st in range(5):
-        sib_arrive(0, st)
-    qwait(0)
-    feed(0, 0)
-    feed(0, -1)
-    feed(0, 1)
-    arrive(1, 3)
-    wfwd(3)
-    feed(0, -2)
-    feed(0, 2)
-    feed(0, -3)
+    feed_rows(0, 0, 1, -2)
     wfwd(2)
-    feed(0, 3)
-    feed(0, 4)
+    sib_arrive(0, 3)
+    feed_rows(0, 0, 2, -3)
     sib_arrive(1, 0)
     sib_arrive(1, 1)
+    feed_rows(1, 0, 0, -1)
+    sib_arrive(0, 4)
+    feed_rows(0, 0, 3, 4)
+    qwait(0)
+    feed_rows(0, 1, 0, -1)
+    feed_rows(0, 1, 1, -2)
+    arrive(1, 3)
+    feed_rows(0, 1, 2, -3)
+    feed_rows(0, 1, 3, 4)
     qwait(1)
-    feed(1, 0)
+    feed_rows(1, 1, 0, -1)
     finish_partner(0)
-    arrive(2, 2)
-    feed(1, -1)
+    wfwd(3)
     feed(1, 1)
     sib_arrive(1, 2)
     feed(1, -2)
     feed(1, 2)
-    arrive(1, 4)
+    arrive(2, 2)
+    wfwd(4)
     sib_arrive(1, 3)
     feed(1, -3)
     feed(1, 3)
-    sib_arrive(1, 4)
-    feed(1, 4)
+    merge(0)
     qwait(2)
     sib_arrive(2, 0)
     sib_arrive(2, 1)
     feed(2, 0)
-    finish_partner(1)
-    merge(0)
-    arrive(2, 3)
+    arrive(1, 4)
     feed(2, -1)
     feed(2, 1)
-    wfwd(4)
+    arrive(2, 3, ALL[:2])
+    sib_arrive(1, 4)
+    feed(1, 4)
     sib_arrive(2, 2)
     feed(2, -2)
+    finish_partner(1)
     feed(2, 2)
+    wfwd(5)
+    arrive(2, 3, ALL[2:])
+    att_relay(0)
     sib_arrive(2, 3)
     feed(2, -3)
     feed(2, 3)
+    arrive(2, 4)
     merge(1)
-    flush()
-    att_relay(0)
-    wfwd(5)
-    arrive(2, 4)
     sib_arrive(2, 4)
     feed(2, 4)
     flush_last()
     att_relay(1)
+    merge(2)
     wfwd2()
-    merge(2)
     att_relay(2)
     wdone()
     out_part(0, True)

time: 80.1 us -> 77.2 us (0.964)
  Pallas kernels: 78.5 us -> 76.3 us
    pallas_call x1, Pallas kernels: 78.5 us -> 76.3 us  [per_device(): pl.pallas_call(body, out_shape=pltpu.VMEM((rows, xcols), BF16), in_specs=...]
where the time goes in v3:
time: 77.2 us; the launch traced here: 77.1 us
  Pallas kernels  76.3 us (99%)
    pallas_call x1, Pallas kernels, per_device(): pl.pallas_call(body, out_shape=pltpu.VMEM((rows, xcols), BF16), in_specs=...  76.3 us

profile of v3, /device:TPU:1, one launch (start us, length us, event | category | flops | bytes accessed | tf_op | source)
XLA Modules:
  0.0 77.1 jit_solution(11450499571689868877)
XLA Ops:
  0.0 76.3 %shard_map.64 = bf16[256,640]{1,0:T(8,128)(2,1)S(1)} custom-call(bf16[256,640]{1,0:T(8,128)(2,1)} %x_hbm.1, f32[1,5120]{1,0:T(1,128)} %bitcast.5, bf16[8,640,384]{2,1,0:T(8,128)(2,1)} %bitcast.3, bf16[3,128,5120]{2,1,0:T(8,128)(2,1)} %bitcast.4, bf16[384,384]{1,0:T(8,128)(2,1)} %k_hbm.1, bf16[384,384]{1,0:T(8,128)(2,1)} %v_hbm.1), custom_call_target="tpu_custom_call" | custom-call | tf_op jit(solution)/shard_map/pallas_call | solution.py:448
  76.4 0.7 copy.8

commit v4 on v3

--- a/solution.py
+++ b/solution.py
@@ -17,7 +17,7 @@
 
 def body(x_hbm, gain_ref, wq_hbm, wo_hbm, k_hbm, v_hbm, out_ref,
          kbuf, vbuf, vtmp, xbuf, wq, wobuf, qacc, ssacc, qbuf, acc, mbuf, lbuf,
-         osend, ssend, orecv, srecv, att, oacc, wst,
+         osend, ssend, psend, tsend, orecv, srecv, att, oacc, wst,
          sbuf, lsem, zss, zrs, bss, brs, xss, xrs, wss, wrs, wbs, wbr, wys, wyr, qss, qrs,
          oss, ors, ass, ars):
     rows, xcols = x_hbm.shape
@@ -41,6 +41,7 @@
 
     sib = (blk + 1 - 2 * c, tp)
     ypart = (blk + 2 * NZ - 4 * NZ * yl, tp)
+    ydiag = (blk + 2 * NZ - 4 * NZ * yl, tp + 1 - 2 * yh)
     zsrc = lambda d: lax.rem(z + d + NZ, NZ)
     DX = (1, 3, 2)
     sends = []
@@ -79,7 +80,7 @@
     wol.start()
 
     bar = pltpu.get_barrier_semaphore()
-    peers = [zdev(1), zdev(-1), sib, ypart, tpdev(0, 1)] + [tpdev(dx, 0) for dx in DX]
+    peers = [zdev(1), zdev(-1), sib, ypart, ydiag, tpdev(0, 1)] + [tpdev(dx, 0) for dx in DX]
     for dev in peers:
         pl.semaphore_signal(bar, inc=1, device_id=dev, device_id_type=MESH)
     pl.semaphore_wait(bar, len(peers))
@@ -208,6 +209,7 @@
             update(h, r, sbuf[2 * par + i], values(h, zsrc(d)))
             if i == 0:
                 finish_partner(h)
+        finish_own(h)
 
     def scores(h, zz, r):
         return lax.dot_general(kbuf[h, zz], qbuf[h, r], (((1,), (1,)), ((), ())), preferred_element_type=F32)
@@ -219,20 +221,41 @@
         osend[h] = acc[h, 1].astype(BF16)
         ssend[h, 0:1] = mbuf[h, 1]
         ssend[h, 1:2] = lbuf[h, 1]
-        send(osend.at[h], orecv.at[h], oss.at[h, 0], ors.at[h, 0], ypart)
-        send(ssend.at[h], srecv.at[h], oss.at[h, 1], ors.at[h, 1], ypart)
-
-    def merge(h):
-        await_recv(orecv.at[h], oss.at[h, 0], ors.at[h, 0])
-        await_recv(srecv.at[h], oss.at[h, 1], ors.at[h, 1])
-        ma, mb = mbuf[h, 0], srecv[h, 0:1]
+        send(ssend.at[h], srecv.at[h, 0], oss.at[h, 0], ors.at[h, 0], ypart)
+        send(osend.at[h], orecv.at[h, 0], oss.at[h, 1], ors.at[h, 1], ypart)
+        send(ssend.at[h], srecv.at[h, 1], oss.at[h, 2], ors.at[h, 2], ydiag)
+        send(osend.at[h], orecv.at[h, 1], oss.at[h, 3], ors.at[h, 3], ydiag)
+
+    def finish_own(h):
+        psend[h] = acc[h, 0].astype(BF16)
+        tsend[h, 0:1] = mbuf[h, 0]
+        tsend[h, 1:2] = lbuf[h, 0]
+        send(tsend.at[h], srecv.at[h, 2], oss.at[h, 4], ors.at[h, 4], tpdev(0, 1))
+        send(psend.at[h], orecv.at[h, 2], oss.at[h, 5], ors.at[h, 5], tpdev(0, 1))
+
+    def owait(h, j):
+        await_recv(srecv.at[h, j], oss.at[h, 2 * j], ors.at[h, 2 * j])
+        await_recv(orecv.at[h, j], oss.at[h, 2 * j + 1], ors.at[h, 2 * j + 1])
+
+    def combine(h, t, ma, la, oa, mb, lb, ob):
         m = jnp.maximum(ma, mb)
         fa, fb = jnp.exp2(ma - m), jnp.exp2(mb - m)
-        tot = lbuf[h, 0] * fa + srecv[h, 1:2] * fb
-        o = (acc[h, 0] * fa + orecv[h].astype(F32) * fb) / tot
-        att[h, tp] = o.T.astype(BF16)
-        att_one(h, tp, 3, 0, 1)
+        tot = la * fa + lb * fb
+        att[h, t] = ((oa * fa + ob * fb) / tot).T.astype(BF16)
+
+    def merge(h):
+        owait(h, 0)
+        combine(h, tp, mbuf[h, 0], lbuf[h, 0], acc[h, 0],
+                srecv[h, 0, 0:1], srecv[h, 0, 1:2], orecv[h, 0].astype(F32))
         att_send(h, tp, 0)
+
+    def att_relay(h):
+        owait(h, 1)
+        owait(h, 2)
+        t = tpi(0, 1)
+        combine(h, t, srecv[h, 2, 0:1], srecv[h, 2, 1:2], orecv[h, 2].astype(F32),
+                srecv[h, 1, 0:1], srecv[h, 1, 1:2], orecv[h, 1].astype(F32))
+        att_send(h, t, 4)
 
     def att_one(h, t, i, dx, dy):
         send(att.at[h, t], att.at[h, t], ass.at[h, i], ars.at[h, i], tpdev(dx, dy))
@@ -243,10 +266,6 @@
 
     def att_wait(h, i, dx, dy):
         await_recv(att.at[h, tpi(-dx, dy)], ass.at[h, i], ars.at[h, i])
-
-    def att_relay(h):
-        att_wait(h, 3, 0, 1)
-        att_send(h, tpi(0, 1), 4)
 
     def out_part(h, first=False):
         for i, dx in enumerate(DX):
@@ -388,6 +407,7 @@
     qwait(1)
     feed_rows(1, 1, 0, -1)
     finish_partner(0)
+    finish_own(0)
     wfwd(3)
     feed(1, 1)
     sib_arrive(1, 2)
@@ -412,6 +432,7 @@
     sib_arrive(2, 2)
     feed(2, -2)
     finish_partner(1)
+    finish_own(1)
     feed(2, 2)
     wfwd(5)
     arrive(2, 3, ALL[2:])
@@ -467,6 +488,8 @@
             vm((heads, 8, rows), F32),
             vm((heads, HD, rows), BF16),
             vm((heads, 8, rows), F32),
+            vm((heads, 3, HD, rows), BF16),
+            vm((heads, 3, 8, rows), F32),
             vm((heads, 8, rows, HD), BF16),
             vm((rows, xcols), F32),
             vm((3, heads, HD // 4, xcols), BF16),
@@ -479,7 +502,7 @@
             dma((2, 7)), dma((2, 7)),
             dma((7,)), dma((7,)),
             dma((heads,)), dma((heads,)),
-            dma((heads, 2)), dma((heads, 2)),
+            dma((heads, 6)), dma((heads, 6)),
             dma((heads, 7)), dma((heads, 7)),
         ],
         compiler_params=pltpu.CompilerParams(

time: 77.2 us -> 77.7 us (level)
  no operation moved by 1% of the time
where the time goes in v4:
time: 77.7 us; the launch traced here: 77.6 us
  Pallas kernels  76.9 us (99%)
    pallas_call x1, Pallas kernels, per_device(): pl.pallas_call(body, out_shape=pltpu.VMEM((rows, xcols), BF16), in_specs=...  76.9 us

profile of v4, /device:TPU:1, one launch (start us, length us, event | category | flops | bytes accessed | tf_op | source)
XLA Modules:
  0.0 77.6 jit_solution(4478365662888313597)
XLA Ops:
  0.0 76.9 %shard_map.64 = bf16[256,640]{1,0:T(8,128)(2,1)S(1)} custom-call(bf16[256,640]{1,0:T(8,128)(2,1)} %x_hbm.1, f32[1,5120]{1,0:T(1,128)} %bitcast.5, bf16[8,640,384]{2,1,0:T(8,128)(2,1)} %bitcast.3, bf16[3,128,5120]{2,1,0:T(8,128)(2,1)} %bitcast.4, bf16[384,384]{1,0:T(8,128)(2,1)} %k_hbm.1, bf16[384,384]{1,0:T(8,128)(2,1)} %v_hbm.1), custom_call_target="tpu_custom_call" | custom-call | tf_op jit(solution)/shard_map/pallas_call | solution.py:469
  76.9 0.7 copy.8
